TPU v7x, 32 devices: a whole 2x2x4 slice. The times are simulated.
32 devices in a mesh: grp: 8 (over z, y), blk: 4 (over x, core).
Axes of the slice: x: 2, y: 2, z: 4, core: 2. Of those that a mesh axis runs over, the one named last changes fastest.
Arguments:
- query: bfloat16 [4096, 512], P(('grp', 'blk')), may hold values from -6 to 6
- key: bfloat16 [4096, 512], P(('grp', 'blk')), may hold values from -6 to 6
- value: bfloat16 [4096, 512], P(('grp', 'blk')), may hold values from -6 to 6
- gate_u: bfloat16 [4096, 512], P(('grp', 'blk')), may hold values from -6 to 6
- out_grad: bfloat16 [4096, 1024], P(('grp', 'blk')), may hold values from -6 to 6
- lengths: int32 [8], P('grp'), may hold values from 32 to 512
- norm_gain: float32 [512], replicated, may hold values from 0.1 to 1.9
- out_weight: bfloat16 [512, 1024], replicated, may hold values from -0.25 to 0.25
Outputs:
- layer_out: bfloat16 [4096, 1024], P(('grp', 'blk'))
- grad_query: bfloat16 [4096, 512], P(('grp', 'blk'))
- grad_key: bfloat16 [4096, 512], P(('grp', 'blk'))
- grad_value: bfloat16 [4096, 512], P(('grp', 'blk'))
- grad_gate: bfloat16 [4096, 512], P(('grp', 'blk'))
- grad_weight: float32 [512, 1024], P(None, 'blk')
Inputs may be any that keep to these rules, and one draw needn't show every extreme that they name: `lengths`: events of a user at or past its length are padding.
All inputs are finite; a program needn't handle non-finite values.
Results may differ from a plain program's by a relative error of at most 0.009.
Values may be sent and summed in bfloat16 or wider, within the bound.
No kernel may reach another device: no remote copies, remote signals or barrier semaphores. Data moves between devices by JAX's collectives and lax.ppermute only.
A program may use at most 64 MiB of HBM per device.

v0:
```python
import math
import jax
import jax.numpy as jnp
from jax import lax
from jax.sharding import PartitionSpec as P

HEADS = 8
HEAD = 64
EPS = 1e-05


def causal_mask(query_pos, key_pos, length):
    return (
        (key_pos[None, :] <= query_pos[:, None])
        & (query_pos[:, None] < length)
        & (key_pos[None, :] < length)
    )


def over_blocks(total_rows, step_fn, initial):
    size = math.gcd(total_rows, 512)

    def advance(index, carry):
        return step_fn(carry, index * size, size)

    return lax.fori_loop(0, total_rows // size, advance, initial)


def shards(query, key, value, gate_u, out_grad, lengths, norm_gain, out_weight):
    rows = query.shape[0]
    scale = HEAD ** (-0.5)
    length = lengths[0]
    lanes = lax.axis_size("blk")
    position = lax.axis_index("blk")
    first_row = position * rows
    row_pos = first_row + jnp.arange(rows, dtype=jnp.int32)
    total_len = rows * lanes
    query_heads = query.reshape(rows, HEADS, HEAD)
    key_heads = key.reshape(rows, HEADS, HEAD)
    value_heads = value.reshape(rows, HEADS, HEAD)
    zeros = jnp.zeros((rows, HEADS, HEAD), jnp.float32)
    keys_all, values_all = (
        lax.all_gather(key, "blk", axis=0, tiled=True),
        lax.all_gather(value, "blk", axis=0, tiled=True),
    )

    def forward_step(carry, begin, size):
        key_block = lax.dynamic_slice_in_dim(keys_all, begin, size, 0).reshape(size, HEADS, HEAD)
        value_block = lax.dynamic_slice_in_dim(values_all, begin, size, 0).reshape(
            size, HEADS, HEAD
        )
        scores = (
            jnp.einsum("rhd,nhd->hrn", query_heads, key_block, preferred_element_type=jnp.float32)
            * scale
        )
        mask = causal_mask(row_pos, begin + jnp.arange(size, dtype=jnp.int32), length)
        weights = (jax.nn.silu(scores) * mask[None]).astype(jnp.bfloat16)
        return carry + jnp.einsum(
            "hrn,nhd->rhd", weights, value_block, preferred_element_type=jnp.float32
        )

    attended = over_blocks(total_len, forward_step, zeros).reshape(rows, HEADS * HEAD)
    centre = attended - jnp.mean(attended, axis=1, keepdims=True)
    inv_std = lax.rsqrt(jnp.mean(centre * centre, axis=1, keepdims=True) + EPS)
    normed = centre * inv_std
    scaled = normed * norm_gain
    gates = gate_u.astype(jnp.float32)
    mixed = (scaled * gates).astype(jnp.bfloat16)
    layer_out = jnp.dot(mixed, out_weight, preferred_element_type=jnp.float32).astype(jnp.bfloat16)
    mixed_grad = lax.dot_general(
        out_grad, out_weight, (((1,), (1,)), ((), ())), preferred_element_type=jnp.float32
    )
    grad_gate = (mixed_grad * scaled).astype(jnp.bfloat16)
    normed_grad = mixed_grad * gates * norm_gain
    attended_grad = inv_std * (
        normed_grad
        - jnp.mean(normed_grad, axis=1, keepdims=True)
        - normed * jnp.mean(normed_grad * normed, axis=1, keepdims=True)
    )
    attended_grad = attended_grad.astype(jnp.bfloat16)
    grad_heads = attended_grad.reshape(rows, HEADS, HEAD)
    weight_term = lax.dot_general(
        mixed, out_grad, (((0,), (0,)), ((), ())), preferred_element_type=jnp.float32
    )

    def query_step(carry, begin, size):
        key_block = lax.dynamic_slice_in_dim(keys_all, begin, size, 0).reshape(size, HEADS, HEAD)
        value_block = lax.dynamic_slice_in_dim(values_all, begin, size, 0).reshape(
            size, HEADS, HEAD
        )
        scores = (
            jnp.einsum("rhd,nhd->hrn", query_heads, key_block, preferred_element_type=jnp.float32)
            * scale
        )
        mask = causal_mask(row_pos, begin + jnp.arange(size, dtype=jnp.int32), length)
        sigma = jax.nn.sigmoid(scores)
        prob_grad = jnp.einsum(
            "rhd,nhd->hrn", grad_heads, value_block, preferred_element_type=jnp.float32
        )
        score_grad = (prob_grad * sigma * (1.0 + scores * (1.0 - sigma)) * mask[None]).astype(
            jnp.bfloat16
        )
        return carry + jnp.einsum(
            "hrn,nhd->rhd", score_grad, key_block, preferred_element_type=jnp.float32
        )

    grad_query = (
        (over_blocks(total_len, query_step, zeros) * scale)
        .reshape(rows, HEADS * HEAD)
        .astype(jnp.bfloat16)
    )
    query_piece = lax.all_gather(query, "blk", axis=0, tiled=True)
    grad_piece = lax.all_gather(attended_grad, "blk", axis=0, tiled=True)
    count = query_piece.shape[0]

    def inner(acc, begin, size):
        key_acc, value_acc = acc
        query_block = lax.dynamic_slice_in_dim(query_piece, begin, size, 0).reshape(
            size, HEADS, HEAD
        )
        grad_block = lax.dynamic_slice_in_dim(grad_piece, begin, size, 0).reshape(size, HEADS, HEAD)
        scores = (
            jnp.einsum("nhd,rhd->hnr", query_block, key_heads, preferred_element_type=jnp.float32)
            * scale
        )
        mask = causal_mask(begin + jnp.arange(size, dtype=jnp.int32), row_pos, length)
        weights = (jax.nn.silu(scores) * mask[None]).astype(jnp.bfloat16)
        sigma = jax.nn.sigmoid(scores)
        prob_grad = jnp.einsum(
            "nhd,rhd->hnr", grad_block, value_heads, preferred_element_type=jnp.float32
        )
        score_grad = (prob_grad * sigma * (1.0 + scores * (1.0 - sigma)) * mask[None]).astype(
            jnp.bfloat16
        )
        key_acc = key_acc + jnp.einsum(
            "hnr,nhd->rhd", score_grad, query_block, preferred_element_type=jnp.float32
        )
        value_acc = value_acc + jnp.einsum(
            "hnr,nhd->rhd", weights, grad_block, preferred_element_type=jnp.float32
        )
        return (key_acc, value_acc)

    key_acc, value_acc = over_blocks(count, inner, (zeros, zeros))
    grad_key = (key_acc * scale).reshape(rows, HEADS * HEAD).astype(jnp.bfloat16)
    grad_value = value_acc.reshape(rows, HEADS * HEAD).astype(jnp.bfloat16)
    column_part = lax.psum_scatter(weight_term, "blk", scatter_dimension=1, tiled=True)
    grad_weight = lax.psum(column_part, "grp")
    return (layer_out, grad_query, grad_key, grad_value, grad_gate, grad_weight)


def solution(mesh):
    return jax.shard_map(
        shards,
        mesh=mesh,
        in_specs=(
            P(("grp", "blk"), None),
            P(("grp", "blk"), None),
            P(("grp", "blk"), None),
            P(("grp", "blk"), None),
            P(("grp", "blk"), None),
            P("grp"),
            P(),
            P(),
        ),
        out_specs=(
            P(("grp", "blk"), None),
            P(("grp", "blk"), None),
            P(("grp", "blk"), None),
            P(("grp", "blk"), None),
            P(("grp", "blk"), None),
            P(None, "blk"),
        ),
        check_vma=False,
    )
```

profile of v0, /device:TPU:0, one launch (start us, length us, event | category | flops | bytes accessed | tf_op | source)
XLA Modules:
  0.0 158.3 jit_solution(8994347896110078273)
XLA Ops:
  7.2 9.0 %all_gather.13 = bf16[512,512]{1,0:T(8,128)(2,1)S(1)} all-gather(bf16[128,512]{1,0:T(8,128)(2,1)} %param.10), channel_id=1, replica_groups=mesh['grp'=8,'blk'=4] {'blk'}, dimensions={0}, use_global_device_ids=true | all-gather | bytes 655360 | tf_op jit(solution)/shard_map/all_gather | solution.py:44
  16.2 1.0 copy.26
  17.2 1.0 copy.24
  18.3 7.5 %all_gather.12 = bf16[512,512]{1,0:T(8,128)(2,1)S(1)} all-gather(bf16[128,512]{1,0:T(8,128)(2,1)} %param.9), channel_id=1, replica_groups=mesh['grp'=8,'blk'=4] {'blk'}, dimensions={0}, use_global_device_ids=true | all-gather | bytes 655360 | tf_op jit(solution)/shard_map/all_gather | solution.py:43
  25.7 1.0 copy.25
  27.5 1.5 fusion.33
  29.0 0.1 fusion.19
  29.1 2.0 %fusion.32 = (f32[128]{0:T(128)S(1)}, f32[8,128,64]{1,2,0:T(8,128)S(1)}) fusion(bf16[512,8,64]{0,2,1:T(8,128)(2,1)} %bitcast.51, f32[8,128,512]{2,1,0:T(8,128)S(1)} %fusion.33, f32[128,512]{1,0:T(8,128)S(1)} %fusion.19), kind=kOutput, calls=%fused_computation.56 | convolution fusion | flops 70844288 | bytes 3146240 | tf_op jit(solution)/shard_map/while/body/eval_jaxpr/hrn,nhd->rhd/dot_general | solution.py:58
  31.3 0.5 add_rsqrt_fusion
  31.9 1.1 copy.27
  33.0 1.6 %fusion.23 = (f32[128]{0:T(128)S(1)}, f32[128]{0:T(128)S(1)}, f32[128,512]{1,0:T(8,128)S(1)}) fusion(f32[512]{0:T(512)S(1)} %copy-done.12, bf16[128,512]{1,0:T(8,128)(2,1)S(1)} %copy-done.9, f32[128]{0:T(128)} %add_rsqrt_fusion, f32[128,512]{1,0:T(8,128)S(1)} %copy.27, f32[128]{0:T(128)S(1)} %broadcast_multiply_fusion.2, bf16[128,1024]{1,0:T(8,128)(2,1)} %param.12, ...), kind=kOutput, calls=%fused_computation.40 | convolution fusion | flops 134741760 | bytes 1970176 | tf_op jit(solution)/shard_map/dot_general | solution.py:70
  34.6 1.8 %multiply_convert_fusion.6 = (bf16[128,512]{1,0:T(8,128)(2,1)}, bf16[128,512]{1,0:T(8,128)(2,1)S(1)}, bf16[128,512]{1,0:T(8,128)(2,1)S(1)}) fusion(f32[128,512]{1,0:T(8,128)S(1)} %get-tuple-element.96, f32[128,512]{1,0:T(8,128)S(1)} %copy.27, f32[512]{0:T(512)S(1)} %copy-done.12, f32[128]{0:T(128)} %add_rsqrt_fusion, f32[128]{0:T(128)S(1)} %broadcast_multiply_fusion.2, ...), kind=kLoop, calls=%fused_computation.28 | loop fusion | flops 983040 | bytes 1052672 | tf_op jit(solution)/shard_map/convert_element_type | solution.py:73
  36.4 0.6 copy-done.1
  37.0 1.8 %fusion.35 = f32[512,1024]{1,0:T(8,128)} fusion(bf16[128,512]{1,0:T(8,128)(2,1)S(1)} %get-tuple-element.93, bf16[128,1024]{1,0:T(8,128)(2,1)S(1)} %copy-done.3), kind=kOutput, calls=%fused_computation.59 | convolution fusion | flops 134217728 | bytes 2490368 | tf_op jit(solution)/shard_map/dot_general | solution.py:82
  38.9 0.8 copy.32
  39.7 0.7 copy.30
  40.6 3.3 %fusion.5 = bf16[8,128,64]{1,2,0:T(8,128)(2,1)} fusion(bf16[512,8,64]{0,2,1:T(8,128)(2,1)} %bitcast.47, f32[8,128,512]{2,1,0:T(8,128)S(1)} %fusion.33, bf16[128,8,64]{0,2,1:T(8,128)(2,1)S(1)} %bitcast.59, bf16[512,8,64]{0,2,1:T(8,128)(2,1)} %bitcast.52, f32[128,512]{1,0:T(8,128)} %copy-done.10), kind=kOutput, calls=%fused_computation.12 | convolution fusion | flops 140115968 | bytes 3670016 | tf_op jit(solution)/shard_map/while/body/eval_jaxpr/hrn,nhd->rhd/dot_general | solution.py:103
  43.9 1.7 %copy.33 = bf16[128,512]{1,0:T(8,128)(2,1)} copy(bf16[128,512]{0,1:T(8,128)(2,1)} %bitcast.58) | data formatting | bytes 262144
  45.6 7.3 %all_gather.15 = bf16[512,512]{1,0:T(8,128)(2,1)S(1)} all-gather(bf16[128,512]{1,0:T(8,128)(2,1)S(1)} %copy-done.7), channel_id=1, replica_groups=mesh['grp'=8,'blk'=4] {'blk'}, dimensions={0}, use_global_device_ids=true | all-gather | bytes 655360 | tf_op jit(solution)/shard_map/all_gather | solution.py:112
  52.8 1.0 copy.31
  53.8 9.5 %all_gather.14 = bf16[512,512]{1,0:T(8,128)(2,1)S(1)} all-gather(bf16[128,512]{1,0:T(8,128)(2,1)S(1)} %get-tuple-element.92), channel_id=1, replica_groups=mesh['grp'=8,'blk'=4] {'blk'}, dimensions={0}, use_global_device_ids=true | all-gather | bytes 655360 | tf_op jit(solution)/shard_map/all_gather | solution.py:113
  63.3 1.0 copy.29
  64.3 0.1 fusion.22
  64.5 1.6 %fusion.34 = f32[8,512,128]{2,1,0:T(8,128)S(1)} fusion(bf16[512,8,64]{0,2,1:T(8,128)(2,1)} %bitcast.48, bf16[128,8,64]{0,2,1:T(8,128)(2,1)S(1)} %bitcast.55), kind=kOutput, calls=%fused_computation.58 | convolution fusion | flops 67108864 | bytes 2752512 | tf_op jit(solution)/shard_map/while/body/eval_jaxpr/nhd,rhd->hnr/dot_general | solution.py:123
  66.2 2.6 %fusion.4 = bf16[8,128,64]{1,2,0:T(8,128)(2,1)S(1)} fusion(bf16[512,8,64]{0,2,1:T(8,128)(2,1)} %bitcast.49, f32[8,512,128]{2,1,0:T(8,128)S(1)} %fusion.34, bf16[512,8,64]{0,2,1:T(8,128)(2,1)} %bitcast.53, bf16[128,8,64]{0,2,1:T(8,128)(2,1)} %bitcast.57, f32[512,128]{1,0:T(8,128)S(1)} %fusion.22), kind=kOutput, calls=%fused_computation.11 | convolution fusion | flops 140115968 | bytes 3670016 | tf_op jit(solution)/shard_map/while/body/eval_jaxpr/hnr,nhd->rhd/dot_general | solution.py:135
  68.8 0.8 copy.34
  69.5 3.2 %reduce-scatter.2.cloned.1.call-done = f32[512,256]{1,0:T(8,128)} async-done(((f32[512,1024]{1,0:T(8,128)}), f32[512,256]{1,0:T(8,128)}) %reduce-scatter.2.cloned.1.call-update) | async-done | bytes 524304 | tf_op jit(solution)/shard_map/reduce_scatter | solution.py:146
  72.7 2.0 %convolution_convert_fusion.1 = bf16[8,64,128]{2,1,0:T(8,128)(2,1)S(1)} fusion(bf16[512,8,64]{0,2,1:T(8,128)(2,1)} %bitcast.54, f32[8,512,128]{2,1,0:T(8,128)S(1)} %fusion.34, f32[512,128]{1,0:T(8,128)} %copy-done.11), kind=kOutput, calls=%fused_computation.13 | convolution fusion | flops 70844416 | bytes 3014656 | tf_op jit(solution)/shard_map/while/body/eval_jaxpr/hnr,nhd->rhd/dot_general | solution.py:138
  74.7 0.8 copy.35
  75.5 1.0 convolution_convert_fusion
  76.5 73.1 %all-reduce.2.cloned.1.call-done = f32[512,256]{1,0:T(8,128)} async-done(((f32[512,256]{1,0:T(8,128)}), f32[512,256]{1,0:T(8,128)}) %all-reduce.2.cloned.1.call-update) | async-done | bytes 524304 | tf_op jit(solution)/shard_map/psum | solution.py:147
  149.6 1.9 %copy.38 = f32[512,256]{1,0:T(8,128)} copy(f32[512,256]{1,0:T(8,128)} %all-reduce.2.cloned.1.call-done) | data formatting | bytes 1048576
  (40 shorter events, 0.5 us)
Async XLA Ops:
  7.2 25.8 %copy-start = (bf16[512,1024]{1,0:T(8,128)(2,1)S(1)}, bf16[512,1024]{1,0:T(8,128)(2,1)}, u32[]{:S(2)}) copy-start(bf16[512,1024]{1,0:T(8,128)(2,1)} %param.15) | copy-start | bytes 3145732
  7.2 65.5 %reduce-scatter.2.cloned.1.call-start = ((), (), s32[]{:S(2)}) async-start(), calls=%async_computation.1 | async-start | bytes 2621440 | tf_op jit(solution)/shard_map/reduce_scatter | solution.py:146
  27.4 3.7 %copy-start.13 = (pred[512]{0:T(512)(128)(4,1)}, pred[512]{0:T(512)(128)(4,1)S(1)}, u32[]{:S(2)}) copy-start(pred[512]{0:T(512)(128)(4,1)S(1)} %iota_compare_fusion.2) | copy-start | bytes 1540
  29.1 2.1 %copy-start.10 = (f32[128,512]{1,0:T(8,128)}, f32[128,512]{1,0:T(8,128)S(1)}, u32[]{:S(2)}) copy-start(f32[128,512]{1,0:T(8,128)S(1)} %fusion.19) | copy-start | bytes 786436
  29.1 3.9 %copy-start.9 = (bf16[128,512]{1,0:T(8,128)(2,1)S(1)}, bf16[128,512]{1,0:T(8,128)(2,1)}, u32[]{:S(2)}) copy-start(bf16[128,512]{1,0:T(8,128)(2,1)} %param.11) | copy-start | bytes 393220
  29.1 3.9 %copy-start.12 = (f32[512]{0:T(512)S(1)}, f32[512]{0:T(512)}, u32[]{:S(2)}) copy-start(f32[512]{0:T(512)} %param.14) | copy-start | bytes 6148
  31.2 0.7 copy-start.4
  33.0 4.0 %copy-start.3 = (bf16[128,1024]{1,0:T(8,128)(2,1)S(1)}, bf16[128,1024]{1,0:T(8,128)(2,1)}, u32[]{:S(2)}) copy-start(bf16[128,1024]{1,0:T(8,128)(2,1)} %param.12) | copy-start | bytes 786436
  36.4 0.6 copy-start.1
  37.0 1.9 %copy-start.5 = (bf16[128,512]{1,0:T(8,128)(2,1)S(1)}, bf16[128,512]{1,0:T(8,128)(2,1)}, u32[]{:S(2)}) copy-start(bf16[128,512]{1,0:T(8,128)(2,1)} %param.9) | copy-start | bytes 393220
  37.0 2.7 %copy-start.6 = (bf16[128,512]{1,0:T(8,128)(2,1)S(1)}, bf16[128,512]{1,0:T(8,128)(2,1)}, u32[]{:S(2)}) copy-start(bf16[128,512]{1,0:T(8,128)(2,1)} %param.10) | copy-start | bytes 393220
  38.9 110.8 %all-reduce.2.cloned.1.call-start = ((), (), s32[]{:S(2)}) async-start(), calls=%async_computation.2 | async-start | bytes 1048576 | tf_op jit(solution)/shard_map/psum | solution.py:147
  40.6 5.0 %copy-start.7 = (bf16[128,512]{1,0:T(8,128)(2,1)S(1)}, bf16[128,512]{1,0:T(8,128)(2,1)}, u32[]{:S(2)}) copy-start(bf16[128,512]{1,0:T(8,128)(2,1)} %param.8) | copy-start | bytes 393220
  43.9 20.5 %copy-start.14 = (pred[512]{0:T(512)(128)(4,1)S(1)}, pred[512]{0:T(512)(128)(4,1)}, u32[]{:S(2)}) copy-start(pred[512]{0:T(512)(128)(4,1)} %copy-done.13) | copy-start | bytes 1540
  43.9 20.6 %copy-start.8 = (bf16[128,512]{0,1:T(8,128)(2,1)S(1)}, bf16[128,512]{0,1:T(8,128)(2,1)}, u32[]{:S(2)}) copy-start(bf16[128,512]{0,1:T(8,128)(2,1)} %copy.32) | copy-start | bytes 393220
  64.5 4.3 %copy-start.11 = (f32[512,128]{1,0:T(8,128)}, f32[512,128]{1,0:T(8,128)S(1)}, u32[]{:S(2)}) copy-start(f32[512,128]{1,0:T(8,128)S(1)} %fusion.22) | copy-start | bytes 786436
  72.7 2.8 %copy-start.2 = (bf16[128,512]{1,0:T(8,128)(2,1)S(1)}, bf16[128,512]{1,0:T(8,128)(2,1)}, u32[]{:S(2)}) copy-start(bf16[128,512]{1,0:T(8,128)(2,1)} %copy-done.1) | copy-start | bytes 393220
Sparse Core Ops, SparseCore 0:
  39.0 33.6 reduce-scatter.1
  76.1 73.4 all-reduce.1
where the time goes:
time: 159 us; the launch traced here: 158 us
  waiting for transfers between devices  76.3 us (48%)
  blocking collectives  33.2 us (21%)
  matrix products  17.5 us (11%)
  between operations  14.9 us (9%)
  local copies, waits for them, and re-layouts  13.7 us (9%)
  other arithmetic  2.64 us (2%)
    psum x1, waiting for transfers between devices, shards(): grad_weight = lax.psum(column_part, 'grp')  73.1 us
    all_gather x1, blocking collectives, shards(): grad_piece = lax.all_gather(attended_grad, 'blk', axis=0, tiled=True)  9.49 us
    all_gather x1, blocking collectives, shards(): lax.all_gather(value, 'blk', axis=0, tiled=True)  8.99 us
    unnamed x37, local copies, waits for them, and re-layouts  8.42 us
    all_gather x1, blocking collectives, shards(): lax.all_gather(key, 'blk', axis=0, tiled=True)  7.49 us
    all_gather x1, blocking collectives, shards(): query_piece = lax.all_gather(query, 'blk', axis=0, tiled=True)  7.27 us
    dot_general x1, matrix products, query_step(): jnp.einsum('hrn,nhd->rhd', score_grad, key_block, preferred_element_type=...  3.29 us
  transfers between devices with their start and end apart: 2, of which 2 were waited for; matrix products, arithmetic and copies ran while one was open for 11% of the time, Pallas kernels for 0%

commit v1 on v0

--- a/solution.py
+++ b/solution.py
@@ -7,6 +7,15 @@
 HEADS = 8
 HEAD = 64
 EPS = 1e-05
+
+
+def open_panel_on(my_data, s0, lane_axis):
+    value_now = jnp.split(
+        lax.all_gather(jnp.concatenate([my_data, s0], axis=1), lane_axis, axis=0, tiled=True),
+        [my_data.shape[1]],
+        axis=1,
+    )
+    return value_now
 
 
 def causal_mask(query_pos, key_pos, length):
@@ -109,8 +118,7 @@
         .reshape(rows, HEADS * HEAD)
         .astype(jnp.bfloat16)
     )
-    query_piece = lax.all_gather(query, "blk", axis=0, tiled=True)
-    grad_piece = lax.all_gather(attended_grad, "blk", axis=0, tiled=True)
+    query_piece, grad_piece = open_panel_on(query, attended_grad, "blk")
     count = query_piece.shape[0]
 
     def inner(acc, begin, size):

time: 159 us -> 175 us (1.10)
  waiting for transfers between devices: 76.3 us -> 107 us
  blocking collectives: 33.2 us -> 16.5 us
    reduce_scatter x1, waiting for transfers between devices: 3.17 us -> 28.9 us  [shards(): lax.psum_scatter(weight_term, 'blk', scatter_dimension=1, tiled=True)]
    all_gather x2 -> x0, blocking collectives: 16.8 us -> none  [the longest x1 9.49 us: shards(): grad_piece = lax.all_gather(attended_grad, 'blk', axis=0, tiled=True)]
    all_gather x0 -> x1, waiting for transfers between devices: none -> 7.79 us  [open_panel_on(): lax.all_gather(jnp.concatenate([my_data, s0], axis=1), lane_axis, axis=0,...]
    split x0 -> x3, local copies, waits for them, and re-layouts: none -> 3.28 us  [open_panel_on(): jnp.split(lax.all_gather(jnp.concatenate([my_data, s0], axis=1), lane_axi...]
    psum x1, waiting for transfers between devices: 73.1 us -> 70.1 us  [shards(): grad_weight = lax.psum(column_part, 'grp')]
    all_gather x2 -> x0, local copies, waits for them, and re-layouts: 2.02 us -> none  [the longest x1 1.02 us: shards(): grad_piece = lax.all_gather(attended_grad, 'blk', axis=0, tiled=True)]
    unnamed x37 -> x29, local copies, waits for them, and re-layouts: 8.42 us -> 6.85 us
  transfers between devices with their start and end apart: 2 -> 3, of which waited for: 2 -> 3; matrix products, arithmetic and copies ran while one was open for 11% -> 12% of each run, Pallas kernels for 0% -> 0%
where the time goes in v1:
time: 175 us; the launch traced here: 174 us
  waiting for transfers between devices  107 us (61%)
  matrix products  17.6 us (10%)
  blocking collectives  16.5 us (9%)
  between operations  14.6 us (8%)
  local copies, waits for them, and re-layouts  14 us (8%)
  other arithmetic  4.32 us (2%)
    psum x1, waiting for transfers between devices, shards(): grad_weight = lax.psum(column_part, 'grp')  70.1 us
    reduce_scatter x1, waiting for transfers between devices, shards(): lax.psum_scatter(weight_term, 'blk', scatter_dimension=1, tiled=True)  28.9 us
    all_gather x1, blocking collectives, shards(): lax.all_gather(value, 'blk', axis=0, tiled=True)  8.99 us
    all_gather x1, waiting for transfers between devices, open_panel_on(): lax.all_gather(jnp.concatenate([my_data, s0], axis=1), lane_axis, axis=0,...  7.79 us
    all_gather x1, blocking collectives, shards(): lax.all_gather(key, 'blk', axis=0, tiled=True)  7.49 us
    unnamed x29, local copies, waits for them, and re-layouts  6.85 us
  transfers between devices with their start and end apart: 3, of which 3 were waited for; matrix products, arithmetic and copies ran while one was open for 12% of the time, Pallas kernels for 0%

profile of v1, /device:TPU:0, one launch (start us, length us, event | category | flops | bytes accessed | tf_op | source)
XLA Modules:
  0.0 173.9 jit_solution(12305118625459041422)
XLA Ops:
  7.2 9.0 %all_gather.10 = bf16[512,512]{1,0:T(8,128)(2,1)S(1)} all-gather(bf16[128,512]{1,0:T(8,128)(2,1)} %param.10), channel_id=1, replica_groups=mesh['grp'=8,'blk'=4] {'blk'}, dimensions={0}, use_global_device_ids=true | all-gather | bytes 655360 | tf_op jit(solution)/shard_map/all_gather | solution.py:53
  16.2 1.0 copy.27
  17.2 1.0 copy.25
  18.3 7.5 %all_gather.9 = bf16[512,512]{1,0:T(8,128)(2,1)S(1)} all-gather(bf16[128,512]{1,0:T(8,128)(2,1)} %param.9), channel_id=1, replica_groups=mesh['grp'=8,'blk'=4] {'blk'}, dimensions={0}, use_global_device_ids=true | all-gather | bytes 655360 | tf_op jit(solution)/shard_map/all_gather | solution.py:52
  25.7 1.0 copy.26
  27.4 1.5 fusion.34
  29.1 2.0 %fusion.33 = (f32[128]{0:T(128)S(1)}, f32[8,128,64]{1,2,0:T(8,128)S(1)}) fusion(bf16[512,8,64]{0,2,1:T(8,128)(2,1)} %bitcast.51, f32[8,128,512]{2,1,0:T(8,128)S(1)} %fusion.34, f32[128,512]{1,0:T(8,128)S(1)} %fusion.19), kind=kOutput, calls=%fused_computation.58 | convolution fusion | flops 70844288 | bytes 3146240 | tf_op jit(solution)/shard_map/while/body/eval_jaxpr/hrn,nhd->rhd/dot_general | solution.py:67
  31.3 0.5 add_rsqrt_fusion
  31.9 1.1 copy.28
  33.0 1.5 fusion.23
  34.5 1.8 %multiply_convert_fusion.6 = (bf16[128,512]{1,0:T(8,128)(2,1)}, bf16[128,512]{1,0:T(8,128)(2,1)S(1)}, bf16[128,512]{1,0:T(8,128)(2,1)}) fusion(f32[128,512]{1,0:T(8,128)S(1)} %get-tuple-element.108, f32[128,512]{1,0:T(8,128)S(1)} %copy.28, f32[512]{0:T(512)S(1)} %copy-done.8, f32[128]{0:T(128)} %add_rsqrt_fusion, f32[128]{0:T(128)S(1)} %broadcast_multiply_fusion.2, ...), kind=kLoop, calls=%fused_computation.29 | loop fusion | flops 983040 | bytes 1052672 | tf_op jit(solution)/shard_map/convert_element_type | solution.py:82
  36.3 1.6 pad_maximum_fusion
  38.1 2.9 %fusion.36 = f32[512,1024]{1,0:T(8,128)} fusion(bf16[128,512]{1,0:T(8,128)(2,1)} %get-tuple-element.95, bf16[128,1024]{1,0:T(8,128)(2,1)} %param.12), kind=kOutput, calls=%fused_computation.61 | convolution fusion | flops 134217728 | bytes 2490368 | tf_op jit(solution)/shard_map/dot_general | solution.py:91
  41.0 0.8 copy.29
  41.8 0.8 copy.33
  42.5 0.8 copy.32
  43.3 2.7 %fusion.5 = bf16[8,128,64]{1,2,0:T(8,128)(2,1)S(1)} fusion(bf16[512,8,64]{0,2,1:T(8,128)(2,1)} %bitcast.47, f32[8,128,512]{2,1,0:T(8,128)S(1)} %fusion.34, bf16[128,8,64]{0,2,1:T(8,128)(2,1)} %bitcast.58, bf16[512,8,64]{0,2,1:T(8,128)(2,1)} %bitcast.52, f32[128,512]{1,0:T(8,128)} %copy-done.7), kind=kOutput, calls=%fused_computation.12 | convolution fusion | flops 140115968 | bytes 3670016 | tf_op jit(solution)/shard_map/while/body/eval_jaxpr/hrn,nhd->rhd/dot_general | solution.py:112
  46.0 0.8 copy.34
  46.7 0.1 fusion.22
  46.9 1.0 convolution_convert_fusion
  47.9 7.8 %all-gather.2.cloned.1.call-done = bf16[512,1024]{1,0:T(8,128)(2,1)} async-done(((bf16[128,1024]{1,0:T(8,128)(2,1)}), bf16[512,1024]{1,0:T(8,128)(2,1)}) %all-gather.2.cloned.1.call-update) | async-done | bytes 1048592 | tf_op jit(solution)/shard_map/all_gather | solution.py:14
  55.7 1.3 fusion.32
  57.0 1.0 copy.30
  58.0 1.0 copy.31
  59.0 1.5 fusion.35
  60.5 28.9 %reduce-scatter.2.cloned.1.call-done = f32[512,256]{1,0:T(8,128)} async-done(((f32[512,1024]{1,0:T(8,128)}), f32[512,256]{1,0:T(8,128)}) %reduce-scatter.2.cloned.1.call-update) | async-done | bytes 524304 | tf_op jit(solution)/shard_map/reduce_scatter | solution.py:154
  89.5 2.6 %fusion.4 = bf16[8,64,128]{2,1,0:T(8,128)(2,1)S(1)} fusion(bf16[512,8,64]{0,2,1:T(8,128)(2,1)} %bitcast.49, f32[8,512,128]{2,1,0:T(8,128)S(1)} %fusion.35, bf16[512,8,64]{0,2,1:T(8,128)(2,1)} %bitcast.53, bf16[128,8,64]{0,2,1:T(8,128)(2,1)} %bitcast.57, f32[512,128]{1,0:T(8,128)S(1)} %fusion.22), kind=kOutput, calls=%fused_computation.11 | convolution fusion | flops 140115968 | bytes 3670016 | tf_op jit(solution)/shard_map/while/body/eval_jaxpr/hnr,nhd->rhd/dot_general | solution.py:143
  92.0 0.8 copy.35
  92.8 1.9 %convolution_convert_fusion.1 = bf16[8,64,128]{2,1,0:T(8,128)(2,1)S(1)} fusion(bf16[512,8,64]{0,2,1:T(8,128)(2,1)} %bitcast.54, f32[8,512,128]{2,1,0:T(8,128)S(1)} %fusion.35, f32[512,128]{1,0:T(8,128)S(1)} %fusion.22), kind=kOutput, calls=%fused_computation.13 | convolution fusion | flops 70844416 | bytes 3014656 | tf_op jit(solution)/shard_map/while/body/eval_jaxpr/hnr,nhd->rhd/dot_general | solution.py:146
  94.7 0.8 copy.36
  95.5 70.1 %all-reduce.2.cloned.1.call-done = f32[512,256]{1,0:T(8,128)} async-done(((f32[512,256]{1,0:T(8,128)}), f32[512,256]{1,0:T(8,128)}) %all-reduce.2.cloned.1.call-update) | async-done | bytes 524304 | tf_op jit(solution)/shard_map/psum | solution.py:155
  165.5 1.9 %copy.39 = f32[512,256]{1,0:T(8,128)} copy(f32[512,256]{1,0:T(8,128)} %all-reduce.2.cloned.1.call-done) | data formatting | bytes 1048576
  (35 shorter events, 0.5 us)
Async XLA Ops:
  7.2 25.8 %copy-start = (bf16[512,1024]{1,0:T(8,128)(2,1)S(1)}, bf16[512,1024]{1,0:T(8,128)(2,1)}, u32[]{:S(2)}) copy-start(bf16[512,1024]{1,0:T(8,128)(2,1)} %param.15) | copy-start | bytes 3145732
  7.2 48.5 %all-gather.2.cloned.1.call-start = ((), (), s32[]{:S(2)}) async-start(), calls=%async_computation.1 | async-start | bytes 1310720 | tf_op jit(solution)/shard_map/all_gather | solution.py:14
  27.4 3.7 %copy-start.9 = (pred[512]{0:T(512)(128)(4,1)}, pred[512]{0:T(512)(128)(4,1)S(1)}, u32[]{:S(2)}) copy-start(pred[512]{0:T(512)(128)(4,1)S(1)} %iota_compare_fusion.2) | copy-start | bytes 1540
  29.1 2.1 %copy-start.7 = (f32[128,512]{1,0:T(8,128)}, f32[128,512]{1,0:T(8,128)S(1)}, u32[]{:S(2)}) copy-start(f32[128,512]{1,0:T(8,128)S(1)} %fusion.19) | copy-start | bytes 786436
  29.1 3.9 %copy-start.6 = (bf16[128,512]{1,0:T(8,128)(2,1)S(1)}, bf16[128,512]{1,0:T(8,128)(2,1)}, u32[]{:S(2)}) copy-start(bf16[128,512]{1,0:T(8,128)(2,1)} %param.11) | copy-start | bytes 393220
  29.1 3.9 %copy-start.8 = (f32[512]{0:T(512)S(1)}, f32[512]{0:T(512)}, u32[]{:S(2)}) copy-start(f32[512]{0:T(512)} %param.14) | copy-start | bytes 6148
  31.2 0.7 copy-start.2
  38.0 51.4 %reduce-scatter.2.cloned.1.call-start = ((), (), s32[]{:S(2)}) async-start(), calls=%async_computation.2 | async-start | bytes 2621440 | tf_op jit(solution)/shard_map/reduce_scatter | solution.py:154
  38.1 3.7 %copy-start.3 = (bf16[128,512]{1,0:T(8,128)(2,1)S(1)}, bf16[128,512]{1,0:T(8,128)(2,1)}, u32[]{:S(2)}) copy-start(bf16[128,512]{1,0:T(8,128)(2,1)} %param.9) | copy-start | bytes 393220
  38.1 4.5 %copy-start.4 = (bf16[128,512]{1,0:T(8,128)(2,1)S(1)}, bf16[128,512]{1,0:T(8,128)(2,1)}, u32[]{:S(2)}) copy-start(bf16[128,512]{1,0:T(8,128)(2,1)} %param.10) | copy-start | bytes 393220
  41.0 124.6 %all-reduce.2.cloned.1.call-start = ((), (), s32[]{:S(2)}) async-start(), calls=%async_computation.3 | async-start | bytes 1048576 | tf_op jit(solution)/shard_map/psum | solution.py:155
  43.3 3.5 %copy-start.10 = (pred[512]{0:T(512)(128)(4,1)S(1)}, pred[512]{0:T(512)(128)(4,1)}, u32[]{:S(2)}) copy-start(pred[512]{0:T(512)(128)(4,1)} %copy-done.9) | copy-start | bytes 1540
  43.3 3.6 %copy-start.1 = (bf16[128,512]{1,0:T(8,128)(2,1)S(1)}, bf16[128,512]{1,0:T(8,128)(2,1)}, u32[]{:S(2)}) copy-start(bf16[128,512]{1,0:T(8,128)(2,1)} %get-tuple-element.95) | copy-start | bytes 393220
  47.9 11.1 %copy-start.5 = (bf16[128,512]{0,1:T(8,128)(2,1)S(1)}, bf16[128,512]{0,1:T(8,128)(2,1)}, u32[]{:S(2)}) copy-start(bf16[128,512]{0,1:T(8,128)(2,1)} %copy.33) | copy-start | bytes 393220
Sparse Core Ops, SparseCore 0:
  38.1 17.5 all-gather.1
  58.2 31.1 reduce-scatter.1
  92.9 72.6 all-reduce.1
